TPU v7x, 32 devices: a whole 2x2x4 slice. The times are simulated.
32 devices in a mesh: client: 8 (over z, x), head: 4 (over y, core).
Axes of the slice: x: 2, y: 2, z: 4, core: 2. Of those that a mesh axis runs over, the one named last changes fastest.
Arguments:
- pre: bfloat16 [10240, 4096], P('client'), may hold values from -40 to 40
- delta: float32 [10240, 4096], P('client', 'head'), may hold values from -300 to 300
- head_weight: bfloat16 [4096, 4096], P(None, 'head'), may hold values from -0.09375 to 0.09375
- client_ids: int32 [128], P('client'), may hold values from 0 to 127, as said below
Outputs:
- head_grad: float32 [4096, 4096], P('client', 'head')
- bias_grad: float32 [4096], P('head')
- embed_grad: float32 [128, 4096], P('client', 'head')
- span_grad: float32 [80, 4096], P(None, 'head')
Inputs may be any that keep to these rules, and one draw needn't show every extreme that they name: `client_ids`: each of the 128 clients appears exactly once.
All inputs are finite; a program needn't handle non-finite values.
Results may differ from a plain program's by a relative error of at most 0.024.
Values may be sent and summed in bfloat16 or wider, within the bound.
A program may use at most 128 MiB of HBM per device.

v0:
```python
import jax
import jax.numpy as jnp
from jax import lax
from jax.sharding import PartitionSpec as P

EPSILON = 1e-06


def silu_slope(values):
    sigma = jax.nn.sigmoid(values)
    return sigma * (1.0 + values * (1.0 - sigma))


def clip_factor(total, number):
    return jnp.minimum(1.0, 1.0 / jnp.sqrt(total / number + EPSILON))


def per_device(pre, delta, head_weight, client_ids):
    rows_here, hidden_width = pre.shape
    emit_here = delta.shape[1]
    clients_here = client_ids.shape[0]
    span_count = rows_here // clients_here
    head_devices = lax.axis_size("head")
    client_devices = lax.axis_size("client")
    hidden = jax.nn.silu(pre.astype(jnp.float32)).astype(jnp.bfloat16)
    delta_low = delta.astype(jnp.bfloat16)
    head_raw = lax.psum_scatter(
        lax.dot_general(
            hidden, delta_low, (((0,), (0,)), ((), ())), preferred_element_type=jnp.float32
        ).astype(jnp.bfloat16),
        "client",
        scatter_dimension=0,
        tiled=True,
    ).astype(jnp.float32)
    head_square = jnp.sum(head_raw * head_raw)
    head_square = lax.psum(head_square, ("client", "head"))
    bias_local = jnp.sum(delta, axis=0)
    partial_sum = lax.dot_general(
        delta_low, head_weight, (((1,), (1,)), ((), ())), preferred_element_type=jnp.float32
    )
    rounded = lax.optimization_barrier(partial_sum.astype(jnp.bfloat16))
    block_grad = rounded.astype(jnp.float32) * silu_slope(pre.astype(jnp.float32))
    grouped = block_grad.reshape(clients_here, span_count, hidden_width)
    client_whole = jnp.sum(grouped, axis=1)
    span_whole = jnp.sum(grouped, axis=0)
    client_part, span_part = (
        lax.psum_scatter(
            client_whole.astype(jnp.bfloat16), "head", scatter_dimension=1, tiled=True
        ).astype(jnp.float32),
        lax.psum_scatter(
            span_whole.astype(jnp.bfloat16), "head", scatter_dimension=1, tiled=True
        ).astype(jnp.float32),
    )
    span_raw, bias_raw = (
        lax.psum(span_part.astype(jnp.bfloat16), "client").astype(jnp.float32),
        lax.psum(bias_local.astype(jnp.bfloat16), "client").astype(jnp.float32),
    )
    targets = lax.iota(jnp.int32, lax.axis_size("client") * clients_here)
    selector = (targets[:, None] == client_ids[None, :]).astype(jnp.float32)
    embed_raw = lax.psum_scatter(
        jnp.dot(
            selector,
            client_part,
            precision=lax.Precision.HIGHEST,
            preferred_element_type=jnp.float32,
        ).astype(jnp.bfloat16),
        "client",
        scatter_dimension=0,
        tiled=True,
    ).astype(jnp.float32)
    leading = (lax.axis_index("client") == 0).astype(jnp.float32)
    small_square = leading * (jnp.sum(span_raw * span_raw) + jnp.sum(bias_raw * bias_raw))
    embed_square = jnp.sum(embed_raw * embed_raw)
    embed_total, small_total = lax.psum((embed_square, small_square), ("client", "head"))
    emit_total = emit_here * head_devices
    clients_total = clients_here * client_devices
    head_factor = clip_factor(head_square, hidden_width * emit_total)
    embed_factor = clip_factor(embed_total, clients_total * hidden_width)
    rest_factor = clip_factor(small_total, span_count * hidden_width + emit_total)
    return (
        head_factor * head_raw,
        rest_factor * bias_raw,
        embed_factor * embed_raw,
        rest_factor * span_raw,
    )


def solution(mesh):
    placed = (P("client", None), P("client", "head"), P(None, "head"), P("client"))
    return jax.shard_map(
        per_device,
        mesh=mesh,
        in_specs=placed,
        out_specs=(P("client", "head"), P("head"), P("client", "head"), P(None, "head")),
        check_vma=False,
    )
```

profile of v0, /device:TPU:0, one launch (start us, length us, event | category | flops | bytes accessed | tf_op | source)
XLA Modules:
  0.0 433.6 jit_solution(12990887152646815512)
XLA Ops:
  7.2 0.0 reduce-scatter.9.cloned.1.call-start
  7.2 0.0 copy-start
  7.2 17.6 %convolution_convert_fusion = bf16[1280,4096]{1,0:T(8,128)(2,1)} fusion(bf16[4096,1024]{1,0:T(8,128)(2,1)} %param.6, f32[1280,1024]{1,0:T(8,128)} %param.5), kind=kOutput, calls=%fused_computation.10 | convolution fusion | flops 10743971840 | bytes 24117248 | tf_op jit(solution)/shard_map/dot_general | solution.py:38
  24.8 0.0 copy-done
  24.8 9.6 %fusion.6 = f32[1280,4096]{1,0:T(8,128)S(1)} fusion(bf16[1280,4096]{1,0:T(8,128)(2,1)S(1)} %copy-done, bf16[1280,4096]{1,0:T(8,128)(2,1)} %convolution_convert_fusion), kind=kLoop, calls=%fused_computation.9 | loop fusion | flops 52428800 | bytes 41943040 | tf_op jit(solution)/shard_map/mul | solution.py:42
  34.4 0.0 copy-start.1
  34.4 5.2 %fusion.20 = (bf16[16,4096]{1,0:T(8,128)(2,1)}, bf16[80,4096]{1,0:T(8,128)(2,1)}) fusion(f32[16,80,4096]{2,1,0:T(8,128)S(1)} %bitcast.3), kind=kLoop, calls=%fused_computation.31 | loop fusion | flops 10092544 | bytes 21757952 | tf_op jit(solution)/shard_map/reduce_sum | solution.py:44
  39.5 0.0 reduce-scatter.9.cloned.1.call-update
  39.6 0.0 reduce-scatter.7.cloned.1.call-start
  39.6 0.7 reduce-scatter.7.cloned.1.call-update
  40.3 0.0 reduce-scatter.11.cloned.1.call-start
  40.4 21.7 %reduce-scatter.9.cloned.1.call-done = bf16[16,1024]{1,0:T(8,128)(2,1)} async-done(((bf16[16,4096]{1,0:T(8,128)(2,1)}), bf16[16,1024]{1,0:T(8,128)(2,1)}) %reduce-scatter.9.cloned.1.call-update) | async-done | bytes 32784 | tf_op jit(solution)/shard_map/reduce_scatter | solution.py:47
  62.1 0.0 copy-done.1
  62.1 1.7 convolution_convert_fusion.1
  63.7 0.0 reduce-scatter.11.cloned.1.call-update
  63.8 0.0 all-reduce.3.cloned.1.call-start
  63.8 23.8 %reduce-scatter.7.cloned.1.call-done = bf16[80,1024]{1,0:T(8,128)(2,1)} async-done(((bf16[80,4096]{1,0:T(8,128)(2,1)}), bf16[80,1024]{1,0:T(8,128)(2,1)}) %reduce-scatter.7.cloned.1.call-update) | async-done | bytes 163856 | tf_op jit(solution)/shard_map/reduce_scatter | solution.py:50
  87.6 0.0 all-reduce.3.cloned.1.call-update
  87.6 0.2 reduce-scatter.5.cloned.1.call-start
  87.9 18.3 %fusion.9 = bf16[4096,1024]{1,0:T(8,128)(2,1)} fusion(bf16[1280,4096]{1,0:T(8,128)(2,1)} %param.4, f32[1280,1024]{1,0:T(8,128)} %param.5), kind=kOutput, calls=%fused_computation.12 | convolution fusion | flops 10774380544 | bytes 24117248 | tf_op jit(solution)/shard_map/dot_general | solution.py:28
  106.1 0.0 reduce-scatter.5.cloned.1.call-update
  106.2 2.9 reduce_sum.66
  109.0 21.5 %psum.37 = bf16[1024]{0:T(1024)(128)(2,1)S(1)} all-reduce(bf16[1024]{0:T(1024)(128)(2,1)S(1)} %reduce_sum.66), channel_id=1, replica_groups=mesh['client'=8,'head'=4] {'client'}, use_global_device_ids=true, to_apply=%region_8.9 | all-reduce | flops 1024 | bytes 4096 | tf_op jit(solution)/shard_map/psum | solution.py:56
  130.5 0.6 fusion.18
  131.1 22.5 %reduce-scatter.11.cloned.1.call-done = bf16[16,1024]{1,0:T(8,128)(2,1)} async-done(((bf16[128,1024]{1,0:T(8,128)(2,1)}), bf16[16,1024]{1,0:T(8,128)(2,1)}) %reduce-scatter.11.cloned.1.call-update) | async-done | bytes 32784 | tf_op jit(solution)/shard_map/reduce_scatter | solution.py:60
  153.6 1.4 fusion.16
  155.0 70.9 %all-reduce.3.cloned.1.call-done = bf16[80,1024]{1,0:T(8,128)(2,1)} async-done(((bf16[80,1024]{1,0:T(8,128)(2,1)}), bf16[80,1024]{1,0:T(8,128)(2,1)}) %all-reduce.3.cloned.1.call-update) | async-done | bytes 163856 | tf_op jit(solution)/shard_map/psum | solution.py:55
  225.9 1.6 fusion.15
  228.8 147.9 %reduce-scatter.5.cloned.1.call-done = bf16[512,1024]{1,0:T(8,128)(2,1)} async-done(((bf16[4096,1024]{1,0:T(8,128)(2,1)}), bf16[512,1024]{1,0:T(8,128)(2,1)}) %reduce-scatter.5.cloned.1.call-update) | async-done | bytes 1048592 | tf_op jit(solution)/shard_map/reduce_scatter | solution.py:27
  376.7 2.4 fusion.12
  379.0 39.5 %all-reduce = (f32[]{:T(128)}, f32[]{:T(128)}, f32[]{:T(128)}) all-reduce(f32[]{:T(128)} %fusion.12, f32[]{:T(128)S(6)} %mul.61, f32[]{:T(128)} %fusion.16), channel_id=1, replica_groups=mesh['client'=8,'head'=4] {'client','head'}, use_global_device_ids=true, to_apply=%region_2.3 | all-reduce | flops 3 | bytes 24 | tf_op jit(solution)/shard_map/psum | solution.py:36
  419.9 0.6 convert_multiply_fusion.8
  421.2 1.7 convert_multiply_fusion.4
  422.9 1.4 convert_multiply_fusion.6
  424.3 2.8 convert_multiply_fusion.2
Async XLA Ops:
  7.2 54.9 %reduce-scatter.9.cloned.1.call-start = ((), (), s32[]{:S(2)}) async-start(), calls=%async_computation.7 | async-start | bytes 163840 | tf_op jit(solution)/shard_map/reduce_scatter | solution.py:47
  7.2 17.6 %copy-start = (bf16[1280,4096]{1,0:T(8,128)(2,1)S(1)}, bf16[1280,4096]{1,0:T(8,128)(2,1)}, u32[]{:S(2)}) copy-start(bf16[1280,4096]{1,0:T(8,128)(2,1)} %param.4) | copy-start | bytes 31457284
  34.4 27.7 %copy-start.1 = (s32[16]{0:T(128)S(1)}, s32[16]{0:T(128)}, u32[]{:S(2)}) copy-start(s32[16]{0:T(128)} %param.7) | copy-start | bytes 196
  39.6 48.0 %reduce-scatter.7.cloned.1.call-start = ((), (), s32[]{:S(2)}) async-start(), calls=%async_computation.5 | async-start | bytes 819200 | tf_op jit(solution)/shard_map/reduce_scatter | solution.py:50
  40.3 113.3 %reduce-scatter.11.cloned.1.call-start = ((), (), s32[]{:S(2)}) async-start(), calls=%async_computation.8 | async-start | bytes 294912 | tf_op jit(solution)/shard_map/reduce_scatter | solution.py:60
  63.8 162.1 %all-reduce.3.cloned.1.call-start = ((), (), s32[]{:S(2)}) async-start(), calls=%async_computation.6 | async-start | bytes 327680 | tf_op jit(solution)/shard_map/psum | solution.py:55
  87.6 289.0 %reduce-scatter.5.cloned.1.call-start = ((), (), s32[]{:S(2)}) async-start(), calls=%async_computation.4 | async-start | bytes 9437184 | tf_op jit(solution)/shard_map/reduce_scatter | solution.py:27
Sparse Core Ops, SparseCore 0:
  39.7 22.3 reduce-scatter.8
  65.1 22.4 reduce-scatter.6
  91.5 62.0 reduce-scatter.10
  156.8 69.0 all-reduce.2
  229.3 147.2 reduce-scatter.4
where the time goes:
time: 434 us
  waiting for transfers between devices  288 us (66%)
  blocking collectives  61 us (14%)
  matrix products  37.5 us (9%)
  other arithmetic  30 us (7%)
  between operations  17.2 us (4%)
    reduce_scatter x1, waiting for transfers between devices, per_device(): lax.psum_scatter(lax.dot_general(hidden, delta_low, (((0,), (0,)), ((), (...  148 us
    psum x1, waiting for transfers between devices, per_device(): lax.psum(span_part.astype(jnp.bfloat16), 'client').astype(jnp.float32)  70.9 us
    psum x1, blocking collectives, per_device(): head_square = lax.psum(head_square, ('client', 'head'))  39.5 us
    reduce_scatter x1, waiting for transfers between devices, per_device(): lax.psum_scatter(span_whole.astype(jnp.bfloat16), 'head', scatter_dimensi...  23.8 us
    reduce_scatter x1, waiting for transfers between devices, per_device(): lax.psum_scatter(jnp.dot(selector, client_part, precision=lax.Precision.H...  22.5 us
    reduce_scatter x1, waiting for transfers between devices, per_device(): lax.psum_scatter(client_whole.astype(jnp.bfloat16), 'head', scatter_dimen...  21.7 us
    psum x1, blocking collectives, per_device(): lax.psum(bias_local.astype(jnp.bfloat16), 'client').astype(jnp.float32)  21.5 us
    dot_general x1, matrix products, per_device(): lax.dot_general(hidden, delta_low, (((0,), (0,)), ((), ())), preferred_el...  18.3 us
  transfers between devices with their start and end apart: 5, of which 5 were waited for; matrix products, arithmetic and copies ran while one was open for 6% of the time, Pallas kernels for 0%

commit v1 on v0

v1 whole, which is shorter than its diff:
```python
import functools

import jax
import jax.numpy as jnp
from jax import lax
from jax.experimental import pallas as pl
from jax.experimental.pallas import tpu as pltpu
from jax.sharding import PartitionSpec as P

EPSILON = 1e-06
MESH = pl.DeviceIdType.MESH
F32 = jnp.float32
BF16 = jnp.bfloat16


def clip_factor(total, number):
    return jnp.minimum(1.0, 1.0 / jnp.sqrt(total / number + EPSILON))


def flip(index, mask, bits):
    out = 0
    for b in range(bits):
        i = (index // 2**b) % 2
        m = (mask // 2**b) % 2
        out = out + (i + m - 2 * i * m) * 2**b
    return out


def kernel(cfg, pre_ref, delta_ref, weight_ref, ids_ref, head_out, rest_out, embed_out, stat_out,
           pre_v, delta_v, low, weight_v, part, landed, small, small_in, mine, span_in, span_all,
           embed_all, ids_all, stat, stat_in, stat_head_in,
           pre_sem, delta_sem, weight_sem, tree_send, tree_recv, head_send, head_recv,
           span_send, span_recv, gather_send, gather_recv, embed_send, embed_recv,
           ids_send, ids_recv, stat_send, stat_recv):
    n, heads, q, piece, groups, spans, clients = cfg
    bits = n.bit_length() - 1
    block = q * piece
    half = n // 2 * q
    pieces = n * q
    me = lax.axis_index("client")
    my_head = lax.axis_index("head")
    emit = low.shape[1]

    barrier = pltpu.get_barrier_semaphore()
    for d in range(1, n):
        pl.semaphore_signal(barrier, inc=1, device_id={"client": lax.rem(me + d, n)}, device_id_type=MESH)
    for d in range(1, heads):
        pl.semaphore_signal(barrier, inc=1, device_id={"head": lax.rem(my_head + d, heads)}, device_id_type=MESH)

    def place(i):
        pos = i // q
        upper = pos // (n // 2)
        mask = n - 2 - 2 * (pos % (n // 2)) + 1 - upper
        row = flip(me, mask, bits) * block + (i % q) * piece
        return pl.multiple_of(row, piece)

    def pre_copy(i):
        return pltpu.make_async_copy(pre_ref.at[:, pl.ds(place(i), piece)], pre_v.at[i], pre_sem.at[i])

    delta_copy = pltpu.make_async_copy(delta_ref, delta_v, delta_sem)
    weight_copy = pltpu.make_async_copy(weight_ref, weight_v, weight_sem)
    delta_copy.start()
    ahead = 3
    for i in range(ahead):
        pre_copy(i).start()

    delta_copy.wait()
    step = 64
    def narrow(r, total):
        rows = pl.ds(pl.multiple_of(r * step, step), step)
        x = delta_v[rows, :]
        low[rows, :] = x.astype(BF16)
        return total + jnp.sum(x.reshape(step // 8, 8, emit), axis=0)
    bias = lax.fori_loop(0, low.shape[0] // step, narrow, jnp.zeros((8, emit), F32))
    bias = jnp.sum(bias, axis=0, keepdims=True)
    pad = groups * 16 - spans
    mine[pl.ds(spans, pad), :] = jnp.where(
        lax.broadcasted_iota(jnp.int32, (pad, emit), 0) == 0, jnp.broadcast_to(bias, (pad, emit)), 0.0
    ).astype(BF16)

    pl.semaphore_wait(barrier, n - 1 + heads - 1)

    def product(i):
        pre_copy(i).wait()
        p = pre_v[i].astype(F32)
        hidden = (p * jax.nn.sigmoid(p)).astype(BF16)
        value = lax.dot_general(hidden, low[...], (((0,), (0,)), ((), ())), preferred_element_type=F32)
        part[pl.ds(place(i), piece), :] = value.astype(BF16)

    def tree_copy(source_row, slot, stage):
        return pltpu.make_async_remote_copy(
            src_ref=part.at[pl.ds(source_row, piece), :], dst_ref=landed.at[slot],
            send_sem=tree_send.at[slot], recv_sem=tree_recv.at[slot],
            device_id={"client": flip(me, 2**stage, bits)}, device_id_type=MESH)

    def first_slot(i):
        return (n // 2 - 1 - i // q) * q + i % q

    def first(i, carry):
        pre_copy(i + ahead).start()
        product(i)
        tree_copy(place(i), first_slot(i), 0).start()
        return carry
    lax.fori_loop(0, half, first, 0)
    weight_copy.start()

    ids_copies = []
    for d in range(1, n):
        copy = pltpu.make_async_remote_copy(
            src_ref=ids_ref, dst_ref=ids_all.at[d],
            send_sem=ids_send.at[d], recv_sem=ids_recv.at[d],
            device_id={"client": lax.rem(me + d, n)}, device_id_type=MESH)
        copy.start()
        ids_copies.append(copy)

    def own(i, carry):
        @pl.when(i + ahead < pieces)
        def _():
            pre_copy(i + ahead).start()
        product(i)
        return carry
    lax.fori_loop(half, pieces, own, 0)
    weight_copy.wait()

    def slope_sums(i, carry):
        p = pre_v[i].astype(F32)
        row = place(i)
        value = lax.dot_general(
            low[...], weight_v[pl.ds(row, piece), :], (((1,), (1,)), ((), ())), preferred_element_type=F32)
        s = jax.nn.sigmoid(p)
        grad = value.astype(BF16).astype(F32) * (s * (1.0 + p * (1.0 - s)))
        grad = grad.reshape(clients, spans, piece)
        to = row // emit
        columns = pl.ds(pl.multiple_of(row % emit, piece), piece)
        small[to, pl.ds(0, spans), columns] = jnp.sum(grad, axis=0).astype(BF16)
        small[to, pl.ds(spans, clients), columns] = jnp.sum(grad, axis=1).astype(BF16)
        return carry

    bases = [0]
    for s in range(bits):
        bases.append(bases[-1] + (n >> (s + 1)) * q)
    later = []

    def combine(mask, sub):
        row = pl.multiple_of(flip(me, mask, bits) * block + sub * piece, piece)
        level = bits if mask == 0 else (mask & -mask).bit_length() - 1
        for s in range(level):
            slot = bases[s] + (mask >> (s + 1)) * q + sub
            tree_copy(row, slot, s).wait_recv()
        def chunk(r, carry):
            rows = min(64, piece)
            at = pl.multiple_of(r * rows, rows)
            total = part[pl.ds(pl.multiple_of(row + at, rows), rows), :].astype(F32)
            for s in range(level):
                slot = bases[s] + (mask >> (s + 1)) * q + sub
                total = total + landed[slot, pl.ds(at, rows), :].astype(F32)
            if mask == 0:
                head_out[pl.ds(pl.multiple_of(sub * piece + at, rows), rows), :] = total
                return carry + jnp.sum((total * total).reshape(rows // 8, 8, emit), axis=0)
            part[pl.ds(pl.multiple_of(row + at, rows), rows), :] = total.astype(BF16)
            return carry
        rows = min(64, piece)
        start = jnp.zeros((8, emit), F32)
        total = lax.fori_loop(0, piece // rows, chunk, start if mask == 0 else 0)
        if mask == 0:
            return total
        slot = bases[level] + (mask >> (level + 1)) * q + sub
        copy = tree_copy(row, slot, level)
        copy.start()
        later.append(copy)

    order = [(mask, sub) for mask in range(n - 2, -1, -2) for sub in range(q)]
    before = order[: 3 * len(order) // 8]
    middle = order[len(before): 3 * len(order) // 4]
    last = order[len(before) + len(middle):]
    for item in before:
        combine(*item)
    at = 0
    for k, item in enumerate(middle):
        upto = pieces * (k + 1) // len(middle)
        lax.fori_loop(at, upto, slope_sums, 0)
        at = upto
        if k == len(middle) - 1:
            head_copies = []
            for d in range(1, heads):
                target = lax.rem(my_head + d, heads)
                copy = pltpu.make_async_remote_copy(
                    src_ref=small.at[target], dst_ref=small_in.at[d - 1],
                    send_sem=head_send.at[d - 1], recv_sem=head_recv.at[d - 1],
                    device_id={"head": target}, device_id_type=MESH)
                copy.start()
                head_copies.append(copy)
        combine(*item)

    for copy in head_copies:
        copy.wait_recv()
    total = small[my_head].astype(F32)
    for d in range(heads - 1):
        total = total + small_in[d].astype(F32)
    mine[pl.ds(0, spans), :] = total[:spans].astype(BF16)
    embed_all[0] = total[spans:].astype(BF16)

    def span_copy(d):
        target = lax.rem(me + d, n)
        return target, pltpu.make_async_remote_copy(
            src_ref=mine.at[pl.ds(pl.multiple_of(lax.rem(target, groups) * 16, 16), 16), :],
            dst_ref=span_in.at[d], send_sem=span_send.at[d], recv_sem=span_recv.at[d],
            device_id={"client": target}, device_id_type=MESH)

    for d in range(1, n):
        target, copy = span_copy(d)
        @pl.when(target < groups)
        def _():
            copy.start()
    embed_copies = []
    for d in range(1, n):
        copy = pltpu.make_async_remote_copy(
            src_ref=embed_all.at[0], dst_ref=embed_all.at[d],
            send_sem=embed_send.at[d], recv_sem=embed_recv.at[d],
            device_id={"client": lax.rem(me + d, n)}, device_id_type=MESH)
        copy.start()
        embed_copies.append(copy)

    head_square = jnp.zeros((8, emit), F32)
    for item in last[: len(last) // 2]:
        value = combine(*item)
        head_square = head_square if value is None else head_square + value

    def gather_copy(d):
        slot = lax.rem(me, groups)
        return pltpu.make_async_remote_copy(
            src_ref=span_all.at[slot], dst_ref=span_all.at[slot],
            send_sem=gather_send.at[d], recv_sem=gather_recv.at[slot],
            device_id={"client": lax.rem(me + d, n)}, device_id_type=MESH)

    @pl.when(me < groups)
    def _():
        for d in range(1, n):
            span_copy(d)[1].wait_recv()
        total = mine[pl.ds(pl.multiple_of(lax.rem(me, groups) * 16, 16), 16), :].astype(F32)
        for d in range(1, n):
            total = total + span_in[d].astype(F32)
        span_all[lax.rem(me, groups)] = total.astype(BF16)
        for d in range(1, n):
            gather_copy(d).start()

    for copy in embed_copies + ids_copies:
        copy.wait_recv()
    wanted = lax.broadcasted_iota(jnp.int32, (clients, 128), 1) + me * clients
    embed_raw = jnp.zeros((clients, emit), F32)
    for d in range(n):
        ids = ids_ref[...] if d == 0 else ids_all[d]
        chosen = (ids == wanted).astype(F32).astype(BF16)
        picked = lax.dot_general(chosen, embed_all[d], (((0,), (0,)), ((), ())), preferred_element_type=F32)
        embed_raw = embed_raw + picked[:clients]
    embed_out[...] = embed_raw
    embed_square = jnp.sum(embed_raw * embed_raw)

    for g in range(groups):
        @pl.when(me != g)
        def _():
            pltpu.make_async_remote_copy(
                src_ref=span_all.at[g], dst_ref=span_all.at[g],
                send_sem=gather_send.at[0], recv_sem=gather_recv.at[g],
                device_id={"client": lax.rem(me + 1, n)}, device_id_type=MESH).wait_recv()
    rest_square = jnp.zeros((), F32)
    for g in range(groups):
        value = span_all[g].astype(F32)
        rest_out[pl.ds(16 * g, 16), :] = value
        rest_square = rest_square + jnp.sum(value * value)

    for item in last[len(last) // 2:]:
        value = combine(*item)
        head_square = head_square if value is None else head_square + value
    head_total = jnp.sum(head_square)

    line = lax.broadcasted_iota(jnp.int32, (8, 128), 0)
    stat[0] = jnp.where(line == 0, head_total, jnp.where(line == 1, embed_square, rest_square / n))
    copies = []
    for d in range(1, n):
        copy = pltpu.make_async_remote_copy(
            src_ref=stat.at[0], dst_ref=stat_in.at[d - 1], send_sem=stat_send.at[d - 1],
            recv_sem=stat_recv.at[d - 1], device_id={"client": lax.rem(me + d, n)}, device_id_type=MESH)
        copy.start()
        copies.append(copy)
    total = stat[0]
    for d, copy in enumerate(copies):
        copy.wait_recv()
        total = total + stat_in[d]
    stat[1] = total
    more = []
    for d in range(1, heads):
        slot = n - 2 + d
        copy = pltpu.make_async_remote_copy(
            src_ref=stat.at[1], dst_ref=stat_head_in.at[d - 1], send_sem=stat_send.at[slot],
            recv_sem=stat_recv.at[slot], device_id={"head": lax.rem(my_head + d, heads)}, device_id_type=MESH)
        copy.start()
        more.append(copy)
    for d, copy in enumerate(more):
        copy.wait_recv()
        total = total + stat_head_in[d]
    stat_out[...] = total

    def sent(i, carry):
        tree_copy(place(i), first_slot(i), 0).wait_send()
        return carry
    lax.fori_loop(0, half, sent, 0)
    for copy in later + head_copies + embed_copies + ids_copies + copies + more:
        copy.wait_send()
    for d in range(1, n):
        target, copy = span_copy(d)
        @pl.when(target < groups)
        def _():
            copy.wait_send()
    @pl.when(me < groups)
    def _():
        for d in range(1, n):
            gather_copy(d).wait_send()


def per_device(n, heads, pre, delta, head_weight, client_ids):
    rows, hidden_width = pre.shape
    emit = delta.shape[1]
    clients = client_ids.shape[0]
    spans = rows // clients
    block = hidden_width // n
    piece = min(256, block)
    q = block // piece
    groups = (spans + 16) // 16
    cfg = (n, heads, q, piece, groups, spans, clients)
    ids = jnp.broadcast_to(client_ids[:, None], (clients, 128))
    hbm = pl.BlockSpec(memory_space=pl.ANY)
    vmem = pl.BlockSpec(memory_space=pltpu.VMEM)
    dma = pltpu.SemaphoreType.DMA
    slots = (n - 1) * q
    head_raw, rest_raw, embed_raw, stats = pl.pallas_call(
        functools.partial(kernel, cfg),
        out_shape=(
            jax.ShapeDtypeStruct((block, emit), F32),
            jax.ShapeDtypeStruct((groups * 16, emit), F32),
            jax.ShapeDtypeStruct((clients, emit), F32),
            jax.ShapeDtypeStruct((8, 128), F32),
        ),
        in_specs=[hbm, hbm, hbm, vmem],
        out_specs=(vmem, vmem, vmem, vmem),
        scratch_shapes=[
            pltpu.VMEM((n * q, rows, piece), BF16),
            pltpu.VMEM((rows, emit), F32),
            pltpu.VMEM((rows, emit), BF16),
            pltpu.VMEM((hidden_width, emit), BF16),
            pltpu.VMEM((hidden_width, emit), BF16),
            pltpu.VMEM((slots, piece, emit), BF16),
            pltpu.VMEM((heads, spans + clients, emit), BF16),
            pltpu.VMEM((heads - 1, spans + clients, emit), BF16),
            pltpu.VMEM((groups * 16, emit), BF16),
            pltpu.VMEM((n, 16, emit), BF16),
            pltpu.VMEM((groups, 16, emit), BF16),
            pltpu.VMEM((n, clients, emit), BF16),
            pltpu.VMEM((n, clients, 128), jnp.int32),
            pltpu.VMEM((2, 8, 128), F32),
            pltpu.VMEM((n - 1, 8, 128), F32),
            pltpu.VMEM((heads - 1, 8, 128), F32),
            dma((n * q,)), dma, dma, dma((slots,)), dma((slots,)),
            dma((heads - 1,)), dma((heads - 1,)),
            dma((n,)), dma((n,)), dma((n,)), dma((groups,)), dma((n,)), dma((n,)),
            dma((n,)), dma((n,)), dma((n + heads - 2,)), dma((n + heads - 2,)),
        ],
        compiler_params=pltpu.CompilerParams(
            collective_id=0, has_side_effects=True, vmem_limit_bytes=60 * 2**20
        ),
        name="clipped_grads",
    )(pre, delta, head_weight, ids)
    head_factor = clip_factor(stats[0, 0], hidden_width * emit * heads)
    embed_factor = clip_factor(stats[1, 0], clients * n * hidden_width)
    rest_factor = clip_factor(stats[2, 0], spans * hidden_width + emit * heads)
    return (
        head_factor * head_raw,
        rest_factor * rest_raw[spans],
        embed_factor * embed_raw,
        rest_factor * rest_raw[:spans],
    )


def solution(mesh):
    placed = (P("client", None), P("client", "head"), P(None, "head"), P("client"))
    return jax.shard_map(
        functools.partial(per_device, mesh.shape["client"], mesh.shape["head"]),
        mesh=mesh,
        in_specs=placed,
        out_specs=(P("client", "head"), P("head"), P("client", "head"), P(None, "head")),
        check_vma=False,
    )
```

time: 434 us -> 149 us (0.34)
  waiting for transfers between devices: 288 us -> 0 us
  Pallas kernels: 0 us -> 135 us
  blocking collectives: 61 us -> 0 us
  matrix products: 37.5 us -> 0 us
  other arithmetic: 30 us -> 7.76 us
  between operations: 17.2 us -> 2.72 us
    reduce_scatter x4 -> x0, waiting for transfers between devices: 216 us -> none  [the longest x1 148 us: per_device(): lax.psum_scatter(lax.dot_general(hidden, delta_low, (((0,), (0,)), ((), (...]
    pallas_call x0 -> x1, Pallas kernels: none -> 135 us  [per_device(): pl.pallas_call(functools.partial(kernel, cfg), out_shape=(jax.ShapeDtypeS...]
    psum x1 -> x0, waiting for transfers between devices: 70.9 us -> none  [per_device(): lax.psum(span_part.astype(jnp.bfloat16), 'client').astype(jnp.float32)]
    psum x2 -> x0, blocking collectives: 61 us -> none  [the longest x1 39.5 us: per_device(): head_square = lax.psum(head_square, ('client', 'head'))]
    dot_general x3 -> x0, matrix products: 37.5 us -> none  [the longest x1 18.3 us: per_device(): lax.dot_general(hidden, delta_low, (((0,), (0,)), ((), ())), preferred_el...]
    reduce_sum x6 -> x0, other arithmetic: 14 us -> none  [the longest x1 5.16 us: per_device(): client_whole = jnp.sum(grouped, axis=1)]
    mul x3 -> x2, other arithmetic: 11.8 us -> 3.08 us  [the longest x1 1.72 us: per_device(): rest_factor * rest_raw[:spans]]
  transfers between devices with their start and end apart: 5 -> 0, of which waited for: 5 -> 0; matrix products, arithmetic and copies ran while one was open for 6% -> 0% of each run, Pallas kernels for 0% -> 0%
where the time goes in v1:
time: 149 us
  Pallas kernels  135 us (91%)
  other arithmetic  7.76 us (5%)
  between operations  2.72 us (2%)
  local copies, waits for them, and re-layouts  2.62 us (2%)
    pallas_call x1, Pallas kernels, per_device(): pl.pallas_call(functools.partial(kernel, cfg), out_shape=(jax.ShapeDtypeS...  135 us
    mul x1, other arithmetic, per_device(): head_factor * head_raw  3.2 us

profile of v1, /device:TPU:0, one launch (start us, length us, event | category | flops | bytes accessed | tf_op | source)
XLA Modules:
  0.0 148.5 jit_solution(6204546828907031662)
XLA Ops:
  0.6 1.3 broadcast_in_dim.2.ids_ref
  2.0 135.4 %clipped_grads.1 = (f32[512,1024]{1,0:T(8,128)}, f32[96,1024]{1,0:T(8,128)}, f32[16,1024]{1,0:T(8,128)}, f32[8,128]{1,0:T(8,128)}) custom-call(bf16[1280,4096]{1,0:T(8,128)(2,1)} %pre_ref.1, f32[1280,1024]{1,0:T(8,128)} %delta_ref.1, bf16[4096,1024]{1,0:T(8,128)(2,1)} %weight_ref.1, s32[16,128]{1,0:T(8,128)} %broadcast_in_dim.2.ids_ref), custom_call_target="tpu_custom_call" | custom-call | tf_op jit(solution)/shard_map/clipped_grads/pallas_call | solution.py:336
  137.4 1.3 fusion
  139.4 1.7 %slice_multiply_fusion = f32[80,1024]{1,0:T(8,128)} fusion(f32[96,1024]{1,0:T(8,128)} %get-tuple-element.10, f32[]{:T(128)} %bitcast.1), kind=kLoop, calls=%fused_computation.1 | loop fusion | flops 81920 | bytes 655364 | tf_op jit(solution)/shard_map/mul | solution.py:380
  141.1 1.4 slice_multiply_fusion.1
  143.2 1.5 broadcast_multiply_fusion.1
  145.3 3.2 %broadcast_multiply_fusion = f32[512,1024]{1,0:T(8,128)} fusion(f32[512,1024]{1,0:T(8,128)} %get-tuple-element.9, f32[]{:T(128)} %bitcast), kind=kLoop, calls=%fused_computation | loop fusion | flops 524288 | bytes 4194308 | tf_op jit(solution)/shard_map/mul | solution.py:377
